TPU v7x, 256 devices: a whole 4x4x8 slice. The times are simulated.
256 devices in a mesh: units: 64 (over x, z, core), expert: 4 (over y).
Axes of the slice: x: 4, y: 4, z: 8, core: 2. Of those that a mesh axis runs over, the one named last changes fastest.
Arguments:
- a_up: float32 [57344, 2048], P(('expert', 'units')), parts along dimension 0, may hold values from -6 to 6
- a_down: float32 [57344, 2048], P(('expert', 'units')), parts along dimension 0, may hold values from -6 to 6
- b_up: float32 [57344, 2048], P(('expert', 'units')), parts along dimension 0, may hold values from -6 to 6
- b_down: float32 [57344, 2048], P(('expert', 'units')), parts along dimension 0, may hold values from -6 to 6
- perm: int32 [57344], P('expert'), parts along dimension 0, may hold values from 0 to 14335, as said below
Outputs:
- merged_up: float32 [57344, 2048], P(('expert', 'units')), parts along dimension 0
- merged_down: float32 [57344, 2048], P(('expert', 'units')), parts along dimension 0
There are 4 independent parts, one for each index of `expert`. A program takes and returns all parts, laid end to end along the dimension named above; each array names one. Nothing has to cross between parts.
Inputs may be any that keep to these rules, and one draw needn't show every extreme that they name: perm names each of the 14336 units once. Cut the units into aligned blocks of 224: of the units of one source block, at most 5 are matched to units of any one destination block, and in every draw some pair of blocks reaches 5. Every source block sends the same list of counts to the destination blocks, in an order that differs from source to source.
All inputs are finite; a program needn't handle non-finite values.
Results may differ from a plain program's by a relative error of at most 0.00002.
Values sent between devices are 32-bit elements; how exact they have to be, the bound alone decides.
No kernel may reach another device: no remote copies, remote signals or barrier semaphores. Data moves between devices by JAX's collectives and lax.ppermute only.
A program may use at most 64 MiB of HBM per device.

v0:
```python
import math

import jax
import jax.numpy as jnp
from jax import lax
from jax.sharding import Mesh
from jax.sharding import PartitionSpec as P

UNITS = ("units_0", "units_1", "units_2")
EXPERT_UNITS = ("expert", "units_0", "units_1", "units_2")


def in_blocks(x, dim, devices):
    before, after = (x.shape[:dim], x.shape[dim + 1 :])
    return jnp.moveaxis(x.reshape(*before, devices, -1, *after), dim, 0)


def laid_out(tiles, dim):
    dims = list(tiles.shape[1:])
    dims[dim] *= tiles.shape[0]
    return jnp.moveaxis(tiles, 0, dim).reshape(dims)


def moved_by_axis(tiles, axes, order):
    dims = [lax.axis_size(a) for a in axes]
    tiles = tiles.reshape(*dims, *tiles.shape[1:])
    for k in order:
        tiles = lax.all_to_all(tiles, axes[k], split_axis=k, concat_axis=k, tiled=True)
    return tiles.reshape(-1, *tiles.shape[len(axes) :])


def two_step_exchange(x, groups, order, split_dim, concat_dim):
    devices = lax.axis_size(groups[0]) * lax.axis_size(groups[1])
    tiles = in_blocks(x, split_dim, devices)
    return laid_out(moved_by_axis(tiles, groups, order), concat_dim)


def on_device(a_up, a_down, b_up, b_down, perm):
    count = lax.axis_size(UNITS)
    me_index = lax.axis_index(UNITS)
    rows = b_up.shape[0]
    width = b_up.shape[1]
    limit = (rows + count - 1) // count + 1
    total = perm.shape[0]
    mine = me_index * rows + jnp.arange(rows, dtype=jnp.int32)
    turns = math.gcd(count, 8)
    block = total // turns
    own_targets = jnp.zeros((rows,), jnp.int32)
    for turn in range(turns):
        segment = perm[turn * block : (turn + 1) * block]
        owners = (turn * block + jnp.arange(block, dtype=jnp.int32)) // rows
        hits = (segment[None, :] == mine[:, None]).astype(jnp.int32)
        own_targets = own_targets + jnp.sum(hits * owners[None, :], axis=1)
    position = jnp.arange(rows, dtype=jnp.int32)
    same_target = (own_targets[None, :] == own_targets[:, None]).astype(jnp.int32)
    before_me = (position[None, :] < position[:, None]).astype(jnp.int32)
    ranking = jnp.sum(same_target * before_me, axis=1)
    keyed = own_targets * limit + ranking
    slot_ids = jnp.arange(count * limit, dtype=jnp.int32)
    matches = (keyed[None, :] == slot_ids[:, None]).astype(jnp.int32)
    slots = jnp.sum(matches * position[None, :], axis=1) + rows * (1 - jnp.sum(matches, axis=1))
    own_sources = lax.dynamic_slice_in_dim(perm, me_index * rows, rows)
    source_dev = own_sources // rows
    same_source = (source_dev[None, :] == source_dev[:, None]).astype(jnp.int32)
    smaller = (own_sources[None, :] < own_sources[:, None]).astype(jnp.int32)
    picks = source_dev * limit + jnp.sum(same_source * smaller, axis=1)

    def pack(matrix):
        return jnp.take(matrix, slots, axis=0, mode="fill", fill_value=0.0)

    def unpack(received, own):
        return (own + jnp.take(received, picks, axis=0)) * 0.5

    half = width // 2
    left_up, left_down = (
        two_step_exchange(pack(b_up[:, :half]), (("units_0", "units_1"), "units_2"), (1, 0), 0, 0),
        two_step_exchange(
            pack(b_down[:, :half]), (("units_0", "units_1"), "units_2"), (1, 0), 0, 0
        ),
    )
    right_up, right_down = (
        two_step_exchange(pack(b_up[:, half:]), (("units_0", "units_1"), "units_2"), (1, 0), 0, 0),
        two_step_exchange(
            pack(b_down[:, half:]), (("units_0", "units_1"), "units_2"), (1, 0), 0, 0
        ),
    )
    merged_up = jnp.concatenate(
        [unpack(left_up, a_up[:, :half]), unpack(right_up, a_up[:, half:])], axis=1
    )
    merged_down = jnp.concatenate(
        [unpack(left_down, a_down[:, :half]), unpack(right_down, a_down[:, half:])], axis=1
    )
    return (merged_up, merged_down)


def solution(mesh):
    finer = Mesh(
        mesh.devices.reshape(4, 8, 2, mesh.shape["expert"]),
        ("units_0", "units_1", "units_2", "expert"),
    )
    placed = (
        P(EXPERT_UNITS, None),
        P(EXPERT_UNITS, None),
        P(EXPERT_UNITS, None),
        P(EXPERT_UNITS, None),
        P("expert"),
    )
    return jax.shard_map(
        on_device,
        mesh=finer,
        in_specs=placed,
        out_specs=(P(EXPERT_UNITS, None), P(EXPERT_UNITS, None)),
        check_vma=False,
    )
```

profile of v0, /device:TPU:8, one launch (start us, length us, event | category | flops | bytes accessed | tf_op | source)
XLA Modules:
  0.0 231.1 jit_solution(15262883870053268299)
XLA Ops:
  6.6 2.4 %gather_fusion.2 = f32[320,1024]{1,0:T(8,128)} fusion(f32[224,1024]{1,0:T(8,128)S(1)} %get-tuple-element.27, s32[1024]{0:T(1024)S(1)} %pad_clamp_fusion.1), kind=kCustom, calls=%fused_computation.2.clone | custom fusion | bytes 2622720 | tf_op jit(solution)/shard_map/jit(_take)/gather | solution.py:69
  9.0 3.9 %gather_fusion.6 = f32[320,1024]{1,0:T(8,128)S(1)} fusion(f32[224,1024]{1,0:T(8,128)} %get-tuple-element.25, s32[1024]{0:T(1024)S(1)} %pad_clamp_fusion.1), kind=kCustom, calls=%fused_computation.4.clone | custom fusion | bytes 2622720 | tf_op jit(solution)/shard_map/jit(_take)/gather | solution.py:69
  12.9 2.4 %gather_fusion = f32[320,1024]{1,0:T(8,128)} fusion(f32[224,1024]{1,0:T(8,128)S(1)} %get-tuple-element.26, s32[1024]{0:T(1024)S(1)} %pad_clamp_fusion.1), kind=kCustom, calls=%fused_computation.clone | custom fusion | bytes 2622720 | tf_op jit(solution)/shard_map/jit(_take)/gather | solution.py:69
  15.3 2.4 %gather_fusion.4 = f32[320,1024]{1,0:T(8,128)} fusion(f32[224,1024]{1,0:T(8,128)S(1)} %get-tuple-element.24, s32[1024]{0:T(1024)S(1)} %pad_clamp_fusion.1), kind=kCustom, calls=%fused_computation.3.clone | custom fusion | bytes 2622720 | tf_op jit(solution)/shard_map/jit(_take)/gather | solution.py:69
  17.7 4.5 %broadcast_select_fusion.1 = (f32[320,1024]{1,0:T(8,128)}, f32[320,1024]{1,0:T(8,128)}, f32[320,1024]{1,0:T(8,128)}, f32[320,1024]{1,0:T(8,128)}) fusion(f32[320,1024]{1,0:T(8,128)} %gather_fusion.4, pred[320]{0:T(512)(128)(4,1)S(1)} %get-tuple-element.18, f32[320,1024]{1,0:T(8,128)S(1)} %copy-done.3, f32[320,1024]{1,0:T(8,128)S(1)} %gather_fusion.6, ...), kind=kLoop, calls=%fused_computation.27 | loop fusion | flops 1310720 | bytes 10486080 | tf_op jit(solution)/shard_map/jit(_take)/select_n | solution.py:69
  23.6 1.8 copy.22
  25.5 3.6 %all-to-all-start.2 = ((f32[32,2,5,1024]{3,0,2,1:T(8,128)}), f32[32,2,5,1024]{3,0,2,1:T(8,128)S(1)}, u32[]{:S(2)}, u32[]{:S(2)}) async-start(f32[32,2,5,1024]{3,0,2,1:T(8,128)} %copy.22), calls=%async_computation.2 | async-start | bytes 2621440 | tf_op jit(solution)/shard_map/all_to_all | solution.py:28
  30.5 1.8 copy.28
  33.7 1.8 copy.19
  38.8 4.5 %all-to-all-start.6 = ((f32[32,2,5,1024]{3,0,2,1:T(8,128)}), f32[32,2,5,1024]{3,0,2,1:T(8,128)}, u32[]{:S(2)}, u32[]{:S(2)}) async-start(f32[32,2,5,1024]{3,0,2,1:T(8,128)} %copy.28), calls=%async_computation.6 | async-start | bytes 2621440 | tf_op jit(solution)/shard_map/all_to_all | solution.py:28
  43.3 2.1 copy.23
  45.8 5.7 %all_to_all.40 = f32[32,2,5,1024]{3,0,2,1:T(8,128)} all-to-all(f32[32,2,5,1024]{3,0,2,1:T(8,128)S(1)} %copy-done.1), channel_id=1, replica_groups=mesh['units_0'=4,'units_1'=8,'units_2'=2,'expert'=4] {'units_2'}, dimensions={1} | all-to-all | bytes 2621440 | tf_op jit(solution)/shard_map/all_to_all | solution.py:28
  51.5 5.6 %all_to_all.41 = f32[32,2,5,1024]{3,0,2,1:T(8,128)} all-to-all(f32[32,2,5,1024]{3,0,2,1:T(8,128)S(1)} %copy-done.2), channel_id=1, replica_groups=mesh['units_0'=4,'units_1'=8,'units_2'=2,'expert'=4] {'units_2'}, dimensions={1} | all-to-all | bytes 2621440 | tf_op jit(solution)/shard_map/all_to_all | solution.py:28
  57.1 11.3 %all-to-all-start.3 = ((f32[32,2,5,1024]{3,1,2,0:T(2,128)}), f32[32,2,5,1024]{3,1,2,0:T(2,128)S(1)}, u32[]{:S(2)}, u32[]{:S(2)}) async-start(f32[32,2,5,1024]{3,1,2,0:T(2,128)} %copy.23), calls=%async_computation.3 | async-start | bytes 2621440 | tf_op jit(solution)/shard_map/all_to_all | solution.py:28
  68.4 3.4 %copy.29 = f32[32,2,5,1024]{3,1,2,0:T(2,128)} copy(f32[32,2,5,1024]{3,0,2,1:T(8,128)} %all-to-all-done.6) | data formatting | bytes 2621440 | tf_op jit(solution)/shard_map/all_to_all | solution.py:28
  71.8 30.9 %all-to-all-done.3 = f32[32,2,5,1024]{3,1,2,0:T(2,128)S(1)} async-done(((f32[32,2,5,1024]{3,1,2,0:T(2,128)}), f32[32,2,5,1024]{3,1,2,0:T(2,128)S(1)}, u32[]{:S(2)}, u32[]{:S(2)}) %all-to-all-start.3) | async-done | bytes 1310752 | tf_op jit(solution)/shard_map/all_to_all | solution.py:28
  102.7 5.3 %all-to-all-start.7 = ((f32[32,2,5,1024]{3,1,2,0:T(2,128)}), f32[32,2,5,1024]{3,1,2,0:T(2,128)S(1)}, u32[]{:S(2)}, u32[]{:S(2)}) async-start(f32[32,2,5,1024]{3,1,2,0:T(2,128)} %copy.29), calls=%async_computation.7 | async-start | bytes 2621440 | tf_op jit(solution)/shard_map/all_to_all | solution.py:28
  108.1 3.4 %copy.20 = f32[32,2,5,1024]{3,1,2,0:T(2,128)} copy(f32[32,2,5,1024]{3,0,2,1:T(8,128)} %all_to_all.40) | data formatting | bytes 2621440 | tf_op jit(solution)/shard_map/all_to_all | solution.py:28
  111.5 30.2 %all-to-all-done.7 = f32[32,2,5,1024]{3,1,2,0:T(2,128)S(1)} async-done(((f32[32,2,5,1024]{3,1,2,0:T(2,128)}), f32[32,2,5,1024]{3,1,2,0:T(2,128)S(1)}, u32[]{:S(2)}, u32[]{:S(2)}) %all-to-all-start.7) | async-done | bytes 1310752 | tf_op jit(solution)/shard_map/all_to_all | solution.py:28
  142.7 5.3 %all-to-all-start.1 = ((f32[32,2,5,1024]{3,1,2,0:T(2,128)}), f32[32,2,5,1024]{3,1,2,0:T(2,128)}, u32[]{:S(2)}, u32[]{:S(2)}) async-start(f32[32,2,5,1024]{3,1,2,0:T(2,128)} %copy.20), calls=%async_computation.1 | async-start | bytes 2621440 | tf_op jit(solution)/shard_map/all_to_all | solution.py:28
  148.1 3.4 %copy.26 = f32[32,2,5,1024]{3,1,2,0:T(2,128)} copy(f32[32,2,5,1024]{3,0,2,1:T(8,128)} %all_to_all.41) | data formatting | bytes 2621440 | tf_op jit(solution)/shard_map/all_to_all | solution.py:28
  151.4 30.2 %all-to-all-done.1 = f32[32,2,5,1024]{3,1,2,0:T(2,128)} async-done(((f32[32,2,5,1024]{3,1,2,0:T(2,128)}), f32[32,2,5,1024]{3,1,2,0:T(2,128)}, u32[]{:S(2)}, u32[]{:S(2)}) %all-to-all-start.1) | async-done | bytes 1310752 | tf_op jit(solution)/shard_map/all_to_all | solution.py:28
  181.7 5.3 %all-to-all-start.5 = ((f32[32,2,5,1024]{3,1,2,0:T(2,128)}), f32[32,2,5,1024]{3,1,2,0:T(2,128)}, u32[]{:S(2)}, u32[]{:S(2)}) async-start(f32[32,2,5,1024]{3,1,2,0:T(2,128)} %copy.26), calls=%async_computation.5 | async-start | bytes 2621440 | tf_op jit(solution)/shard_map/all_to_all | solution.py:28
  188.9 3.2 %copy.30 = f32[32,2,5,1024]{3,2,1,0:T(8,128)} copy(f32[32,2,5,1024]{3,1,2,0:T(2,128)} %copy-done) | data formatting | bytes 2621440 | tf_op jit(solution)/shard_map/all_to_all | solution.py:28
  193.8 1.9 gather_fusion.3
  195.7 1.9 gather_fusion.7
  197.6 1.9 copy.21
  199.7 1.9 gather_fusion.1
  201.7 19.0 %all-to-all-done.5 = f32[32,2,5,1024]{3,1,2,0:T(2,128)} async-done(((f32[32,2,5,1024]{3,1,2,0:T(2,128)}), f32[32,2,5,1024]{3,1,2,0:T(2,128)}, u32[]{:S(2)}, u32[]{:S(2)}) %all-to-all-start.5) | async-done | bytes 1310752 | tf_op jit(solution)/shard_map/all_to_all | solution.py:28
  220.6 1.9 copy.27
  222.8 1.9 gather_fusion.5
  224.7 3.5 %fusion.1 = (f32[224,1024]{1,0:T(8,128)S(1)}, f32[224,1024]{1,0:T(8,128)S(1)}, f32[224,1024]{1,0:T(8,128)S(1)}, f32[224,1024]{1,0:T(8,128)S(1)}) fusion(f32[224,1024]{1,0:T(8,128)} %gather_fusion.5, f32[224,2048]{1,0:T(8,128)} %param.10, pred[224]{0:T(512)(128)(4,1)S(1)} %get-tuple-element.14, f32[224,1024]{1,0:T(8,128)S(1)} %copy-done.5, ...), kind=kLoop, calls=%fused_computation.21 | loop fusion | flops 2752512 | bytes 11010272 | tf_op jit(solution)/shard_map/mul | solution.py:72
  (47 shorter events, 21.5 us)
Async XLA Ops:
  3.4 2.1 copy-start.6
  15.3 2.4 %copy-start.3 = (f32[320,1024]{1,0:T(8,128)S(1)}, f32[320,1024]{1,0:T(8,128)}, u32[]{:S(2)}) copy-start(f32[320,1024]{1,0:T(8,128)} %gather_fusion.2) | copy-start | bytes 3932164
  25.5 13.3 %all-to-all-start.2 = ((f32[32,2,5,1024]{3,0,2,1:T(8,128)}), f32[32,2,5,1024]{3,0,2,1:T(8,128)S(1)}, u32[]{:S(2)}, u32[]{:S(2)}) async-start(f32[32,2,5,1024]{3,0,2,1:T(8,128)} %copy.22), calls=%async_computation.2 | async-start | bytes 2621440 | tf_op jit(solution)/shard_map/all_to_all | solution.py:28
  38.8 6.9 %all-to-all-start.6 = ((f32[32,2,5,1024]{3,0,2,1:T(8,128)}), f32[32,2,5,1024]{3,0,2,1:T(8,128)}, u32[]{:S(2)}, u32[]{:S(2)}) async-start(f32[32,2,5,1024]{3,0,2,1:T(8,128)} %copy.28), calls=%async_computation.6 | async-start | bytes 2621440 | tf_op jit(solution)/shard_map/all_to_all | solution.py:28
  43.3 2.4 %copy-start.1 = (f32[32,2,5,1024]{3,0,2,1:T(8,128)S(1)}, f32[32,2,5,1024]{3,0,2,1:T(8,128)}, u32[]{:S(2)}) copy-start(f32[32,2,5,1024]{3,0,2,1:T(8,128)} %copy.19) | copy-start | bytes 3932164
  45.4 6.0 %copy-start.2 = (f32[32,2,5,1024]{3,0,2,1:T(8,128)S(1)}, f32[32,2,5,1024]{3,0,2,1:T(8,128)}, u32[]{:S(2)}) copy-start(f32[32,2,5,1024]{3,0,2,1:T(8,128)} %copy.25) | copy-start | bytes 3932164
  57.1 45.6 %all-to-all-start.3 = ((f32[32,2,5,1024]{3,1,2,0:T(2,128)}), f32[32,2,5,1024]{3,1,2,0:T(2,128)S(1)}, u32[]{:S(2)}, u32[]{:S(2)}) async-start(f32[32,2,5,1024]{3,1,2,0:T(2,128)} %copy.23), calls=%async_computation.3 | async-start | bytes 2621440 | tf_op jit(solution)/shard_map/all_to_all | solution.py:28
  102.7 39.0 %all-to-all-start.7 = ((f32[32,2,5,1024]{3,1,2,0:T(2,128)}), f32[32,2,5,1024]{3,1,2,0:T(2,128)S(1)}, u32[]{:S(2)}, u32[]{:S(2)}) async-start(f32[32,2,5,1024]{3,1,2,0:T(2,128)} %copy.29), calls=%async_computation.7 | async-start | bytes 2621440 | tf_op jit(solution)/shard_map/all_to_all | solution.py:28
  141.7 1.1 copy-start
  142.7 38.9 %all-to-all-start.1 = ((f32[32,2,5,1024]{3,1,2,0:T(2,128)}), f32[32,2,5,1024]{3,1,2,0:T(2,128)}, u32[]{:S(2)}, u32[]{:S(2)}) async-start(f32[32,2,5,1024]{3,1,2,0:T(2,128)} %copy.20), calls=%async_computation.1 | async-start | bytes 2621440 | tf_op jit(solution)/shard_map/all_to_all | solution.py:28
  181.7 38.9 %all-to-all-start.5 = ((f32[32,2,5,1024]{3,1,2,0:T(2,128)}), f32[32,2,5,1024]{3,1,2,0:T(2,128)}, u32[]{:S(2)}, u32[]{:S(2)}) async-start(f32[32,2,5,1024]{3,1,2,0:T(2,128)} %copy.26), calls=%async_computation.5 | async-start | bytes 2621440 | tf_op jit(solution)/shard_map/all_to_all | solution.py:28
  222.8 1.9 copy-start.4
  222.8 1.9 copy-start.5
where the time goes:
time: 232 us; the launch traced here: 231 us
  waiting for transfers between devices  111 us (48%)
  local copies, waits for them, and re-layouts  59 us (25%)
  starting transfers between devices  35.4 us (15%)
  other arithmetic  13.8 us (6%)
  blocking collectives  11.3 us (5%)
    all_to_all x6, waiting for transfers between devices, moved_by_axis(): lax.all_to_all(tiles, axes[k], split_axis=k, concat_axis=k, tiled=True)  111 us
    all_to_all x6, starting transfers between devices, moved_by_axis(): lax.all_to_all(tiles, axes[k], split_axis=k, concat_axis=k, tiled=True)  35.4 us
    all_to_all x8, local copies, waits for them, and re-layouts, moved_by_axis(): lax.all_to_all(tiles, axes[k], split_axis=k, concat_axis=k, tiled=True)  19.9 us
    another operation x8, local copies, waits for them, and re-layouts, moved_by_axis(): tiles = tiles.reshape(*dims, *tiles.shape[1:])  12.9 us
    all_to_all x2, blocking collectives, moved_by_axis(): lax.all_to_all(tiles, axes[k], split_axis=k, concat_axis=k, tiled=True)  11.3 us
    gather x4, local copies, waits for them, and re-layouts, pack(): return jnp.take(matrix, slots, axis=0, mode='fill', fill_value=0.0)  11.1 us
    gather x4, local copies, waits for them, and re-layouts, unpack(): return (own + jnp.take(received, picks, axis=0)) * 0.5  7.65 us
  transfers between devices with their start and end apart: 6, of which 5 were waited for; matrix products, arithmetic and copies ran while one was open for 16% of the time, Pallas kernels for 0%

commit v1 on v0

v1 whole, which is shorter than its diff:
```python
import functools

import jax
import jax.numpy as jnp
from jax import lax
from jax.experimental import pallas as pl
from jax.experimental.pallas import tpu as pltpu
from jax.sharding import Mesh
from jax.sharding import PartitionSpec as P

UNITS = ("units_0", "units_1", "units_2")
EXCHANGE = ("units_1", "units_2", "units_0")
EXPERT_UNITS = ("expert", "units_0", "units_1", "units_2")
NX, NZ, NC = 4, 8, 2
COUNT = NX * NZ * NC
ROWS = 224
LIMIT = 5
WIDTH = 2048
TALL = WIDTH // 128
BIG = 1 << 24


def unit_of(place):
    return (place % NX) * (NZ * NC) + (place // (NX * NC)) * NC + (place // NX) % NC


def smallest(keys):
    found = []
    for _ in range(LIMIT):
        low = jnp.min(keys, axis=0, keepdims=True)
        found.append(low)
        keys = jnp.where(keys == low, BIG, keys)
    return found


def tables(perm_ref, table_ref):
    me = lax.axis_index(UNITS)
    perm = perm_ref[...]
    unit = lax.broadcasted_iota(jnp.int32, (ROWS, COUNT), 1)
    row = lax.broadcasted_iota(jnp.int32, (ROWS, COUNT), 0)
    local = perm - me * ROWS
    sends = smallest(jnp.where((local >= 0) & (local < ROWS), local, BIG))
    mine = jnp.sum(jnp.where(unit == me, perm, 0), axis=1, keepdims=True)
    local = mine - unit * ROWS
    takes = smallest(jnp.where((local >= 0) & (local < ROWS), local * 256 + row, BIG))
    for r in range(LIMIT):
        table_ref[r : r + 1, 0:COUNT] = jnp.where(sends[r] >= BIG, 0, sends[r])
        table_ref[8 + r : 9 + r, 0:COUNT] = jnp.where(takes[r] >= BIG, ROWS, takes[r] & 255)


def pack_kernel(perm_ref, up_ref, down_ref, send_ref, takes_ref, up, down, table, scalars, sems):
    loads = [
        pltpu.make_async_copy(up_ref, up, sems.at[0]),
        pltpu.make_async_copy(down_ref, down, sems.at[1]),
    ]
    for load in loads:
        load.start()
    tables(perm_ref, table)
    takes_ref[...] = table[8:16, :]
    out = pltpu.make_async_copy(table.at[0:8], scalars, sems.at[2])
    out.start()
    out.wait()
    for load in loads:
        load.wait()

    def fill(place, carry):
        unit = unit_of(place)
        for r in range(LIMIT):
            i = scalars[r, unit]
            start = (i // 8) * (8 * TALL) + i % 8
            at = pl.multiple_of((place * LIMIT + r) * (2 * TALL), 2 * TALL)
            send_ref[pl.ds(at, TALL), :] = up[pl.ds(start, TALL, stride=8), :]
            send_ref[pl.ds(at + TALL, TALL), :] = down[pl.ds(start, TALL, stride=8), :]
        return carry

    lax.fori_loop(0, COUNT, fill, 0)


def unpack_kernel(takes_ref, recv_ref, up_ref, down_ref, out_up, out_down, up, down):
    def place_rows(place, carry):
        unit = unit_of(place)
        for r in range(LIMIT):
            i = takes_ref[r, unit]
            start = (i // 8) * (8 * TALL) + i % 8
            at = pl.multiple_of((place * LIMIT + r) * (2 * TALL), 2 * TALL)
            up[pl.ds(start, TALL, stride=8), :] = recv_ref[pl.ds(at, TALL), :]
            down[pl.ds(start, TALL, stride=8), :] = recv_ref[pl.ds(at + TALL, TALL), :]
        return carry

    lax.fori_loop(0, COUNT, place_rows, 0)
    flat = ROWS * TALL
    out_up[...] = (up_ref[...] + up[0:flat, :]) * 0.5
    out_down[...] = (down_ref[...] + down[0:flat, :]) * 0.5


def tiles_of(x):
    return x.reshape(ROWS // 8, 8, TALL, 128).transpose(0, 2, 1, 3).reshape(ROWS * TALL, 128)


def rows_of(x):
    return x.reshape(ROWS // 8, TALL, 8, 128).transpose(0, 2, 1, 3).reshape(ROWS, WIDTH)


def on_device(a_up, a_down, b_up, b_down, perm):
    flat = ROWS * TALL
    slots = COUNT * LIMIT * 2 * TALL
    vmem = pl.BlockSpec(memory_space=pltpu.VMEM)
    smem = pl.BlockSpec(memory_space=pltpu.SMEM)
    hbm = pl.BlockSpec(memory_space=pl.ANY)
    send, takes = pl.pallas_call(
        pack_kernel,
        name="pack",
        out_shape=(
            jax.ShapeDtypeStruct((slots, 128), jnp.float32),
            jax.ShapeDtypeStruct((8, 128), jnp.int32),
        ),
        in_specs=[vmem, hbm, hbm],
        out_specs=(vmem, vmem),
        scratch_shapes=[
            pltpu.VMEM((flat, 128), jnp.float32),
            pltpu.VMEM((flat, 128), jnp.float32),
            pltpu.VMEM((16, 128), jnp.int32),
            pltpu.SMEM((8, 128), jnp.int32),
            pltpu.SemaphoreType.DMA((3,)),
        ],
    )(perm.reshape(COUNT, ROWS).T, tiles_of(b_up), tiles_of(b_down))
    recv = lax.all_to_all(
        send.reshape(COUNT, LIMIT * 2 * TALL, 128), EXCHANGE, split_axis=0, concat_axis=0, tiled=True
    ).reshape(slots, 128)
    merged_up, merged_down = pl.pallas_call(
        unpack_kernel,
        name="unpack",
        out_shape=(
            jax.ShapeDtypeStruct((flat, 128), jnp.float32),
            jax.ShapeDtypeStruct((flat, 128), jnp.float32),
        ),
        in_specs=[smem, vmem, vmem, vmem],
        out_specs=(vmem, vmem),
        scratch_shapes=[
            pltpu.VMEM((flat + 8 * TALL, 128), jnp.float32),
            pltpu.VMEM((flat + 8 * TALL, 128), jnp.float32),
        ],
    )(takes, recv, tiles_of(a_up), tiles_of(a_down))
    return rows_of(merged_up), rows_of(merged_down)


def solution(mesh):
    finer = Mesh(
        mesh.devices.reshape(NX, NZ, NC, mesh.shape["expert"]),
        ("units_0", "units_1", "units_2", "expert"),
    )
    rows = P(EXPERT_UNITS, None)
    return jax.shard_map(
        on_device,
        mesh=finer,
        in_specs=(rows, rows, rows, rows, P("expert")),
        out_specs=(rows, rows),
        check_vma=False,
    )
```

time: 232 us -> 151 us (0.65)
  blocking collectives: 11.3 us -> 131 us
  waiting for transfers between devices: 111 us -> 0 us
  local copies, waits for them, and re-layouts: 59 us -> 1.65 us
  starting transfers between devices: 35.4 us -> 0 us
  Pallas kernels: 0 us -> 17.8 us
  other arithmetic: 13.8 us -> 0 us
    all_to_all x2 -> x1, blocking collectives: 11.3 us -> 131 us  [on_device(): lax.all_to_all(send.reshape(COUNT, LIMIT * 2 * TALL, 128), EXCHANGE, spli...]
    all_to_all x6 -> x0, waiting for transfers between devices: 111 us -> none  [moved_by_axis(): lax.all_to_all(tiles, axes[k], split_axis=k, concat_axis=k, tiled=True)]
    all_to_all x6 -> x0, starting transfers between devices: 35.4 us -> none  [moved_by_axis(): lax.all_to_all(tiles, axes[k], split_axis=k, concat_axis=k, tiled=True)]
    all_to_all x8 -> x0, local copies, waits for them, and re-layouts: 19.9 us -> none  [moved_by_axis(): lax.all_to_all(tiles, axes[k], split_axis=k, concat_axis=k, tiled=True)]
    gather x8 -> x0, local copies, waits for them, and re-layouts: 18.7 us -> none  [the longest x4 11.1 us: pack(): return jnp.take(matrix, slots, axis=0, mode='fill', fill_value=0.0)]
    pallas_call x0 -> x2, Pallas kernels: none -> 17.8 us  [the longest x1 9.01 us: on_device(): pl.pallas_call(unpack_kernel, name='unpack', out_shape=(jax.ShapeDtypeStr...]
    another operation x12 -> x0, local copies, waits for them, and re-layouts: 15.3 us -> none  [the longest x8 12.9 us: moved_by_axis(): tiles = tiles.reshape(*dims, *tiles.shape[1:])]
    select_n x6 -> x0, other arithmetic: 5.37 us -> none  [the longest x1 4.54 us: pack(): return jnp.take(matrix, slots, axis=0, mode='fill', fill_value=0.0)]
  transfers between devices with their start and end apart: 6 -> 0, of which waited for: 5 -> 0; matrix products, arithmetic and copies ran while one was open for 16% -> 0% of each run, Pallas kernels for 0% -> 0%
where the time goes in v1:
time: 151 us
  blocking collectives  131 us (87%)
  Pallas kernels  17.8 us (12%)
  local copies, waits for them, and re-layouts  1.65 us (1%)
    all_to_all x1, blocking collectives, on_device(): lax.all_to_all(send.reshape(COUNT, LIMIT * 2 * TALL, 128), EXCHANGE, spli...  131 us
    pallas_call x1, Pallas kernels, on_device(): pl.pallas_call(unpack_kernel, name='unpack', out_shape=(jax.ShapeDtypeStr...  9.01 us
    pallas_call x1, Pallas kernels, on_device(): pl.pallas_call(pack_kernel, name='pack', out_shape=(jax.ShapeDtypeStruct(...  8.79 us

profile of v1, /device:TPU:8, one launch (start us, length us, event | category | flops | bytes accessed | tf_op | source)
XLA Modules:
  0.0 150.9 jit_solution(1796646204995388319)
XLA Ops:
  0.6 0.9 reshape.49
  1.5 0.7 copy.7
  2.3 8.8 %pack.1 = (f32[10240,128]{1,0:T(8,128)}, s32[8,128]{1,0:T(8,128)}) custom-call(s32[224,64]{1,0:T(8,128)} %bitcast.39, f32[3584,128]{1,0:T(8,128)} %bitcast.35, f32[3584,128]{1,0:T(8,128)} %bitcast.36), custom_call_target="tpu_custom_call" | custom-call | tf_op jit(solution)/shard_map/pack/pallas_call | solution.py:110
  11.1 130.8 %all_to_all.5 = f32[64,160,128]{2,1,0:T(8,128)} all-to-all(f32[64,160,128]{2,1,0:T(8,128)} %bitcast.34), channel_id=1, replica_groups=mesh['units_0'=4,'units_1'=8,'units_2'=2,'expert'=4] {'units_1','units_2..., dimensions={0} | all-to-all | bytes 10485760 | tf_op jit(solution)/shard_map/all_to_all | solution.py:127
  141.9 9.0 %unpack.1 = (f32[3584,128]{1,0:T(8,128)}, f32[3584,128]{1,0:T(8,128)}) custom-call(s32[8,128]{1,0:T(8,128)} %get-tuple-element.6.takes_ref, f32[10240,128]{1,0:T(8,128)} %bitcast.33, f32[3584,128]{1,0:T(8,128)} %bitcast.37, f32[3584,128]{1,0:T(8,128)} %bitcast.38), custom_call_target="tpu_custom_call" | custom-call | tf_op jit(solution)/shard_map/unpack/pallas_call | solution.py:130

commit v2 on v1

v2 whole, which is shorter than its diff:
```python
import functools

import jax
import jax.numpy as jnp
from jax import lax
from jax.experimental import pallas as pl
from jax.experimental.pallas import tpu as pltpu
from jax.sharding import Mesh
from jax.sharding import PartitionSpec as P

UNITS = ("units_0", "units_1", "units_2")
EXCHANGE = ("units_1", "units_2", "units_0")
EXPERT_UNITS = ("expert", "units_0", "units_1", "units_2")
NX, NZ, NC = 4, 8, 2
COUNT = NX * NZ * NC
ROWS = 224
LIMIT = 5
WIDTH = 2048
TALL = WIDTH // 128
BIG = 1 << 24


def unit_of(x, z, c):
    return x * (NZ * NC) + z * NC + c


def place_of(x, z, c):
    return (z * NC + c) * NX + x


def owner(local):
    return jnp.floor((local.astype(jnp.float32) + 0.5) * (1.0 / ROWS)).astype(jnp.int32)


def send_table(perm, me, table_ref):
    local = perm - me * ROWS
    keys = jnp.where((local >= 0) & (local < ROWS), local, BIG)
    for r in range(LIMIT):
        low = jnp.min(keys, axis=0, keepdims=True)
        table_ref[r : r + 1, 0:COUNT] = jnp.where(low >= BIG, 0, low)
        keys = jnp.where(keys == low, BIG, keys)


def take_table(perm, perm_row, me):
    unit = lax.broadcasted_iota(jnp.int32, (ROWS, COUNT), 1)
    column = jnp.sum(jnp.where(unit == me, perm, 0), axis=1, keepdims=True)
    source = owner(perm_row)
    before = (owner(column) == source) & (column < perm_row)
    rank = jnp.sum(jnp.where(before, 1, 0), axis=0, keepdims=True)
    return place_of(source >> 4, (source >> 1) & 7, source & 1) * LIMIT + rank


def tables_kernel(perm_ref, blocks_ref, sends_ref, takes_ref):
    me = lax.axis_index(UNITS)
    send_table(perm_ref[...], me, sends_ref)
    takes_ref[0:1, 0:ROWS] = take_table(perm_ref[...], blocks_ref[pl.ds(me, 1), :], me)


def pack_kernel(sends_ref, up_ref, down_ref, send_ref):
    def fill(z, carry):
        for c in range(NC):
            for x in range(NX):
                for r in range(LIMIT):
                    i = sends_ref[r, unit_of(x, z, c)]
                    where = pl.ds((i >> 3) * (8 * TALL) + (i & 7), TALL, stride=8)
                    at = pl.multiple_of((place_of(x, z, c) * LIMIT + r) * (2 * TALL), 2 * TALL)
                    send_ref[pl.ds(at, TALL), :] = up_ref[where, :]
                    send_ref[pl.ds(at + TALL, TALL), :] = down_ref[where, :]
        return carry

    lax.fori_loop(0, NZ, fill, 0)


def unpack_kernel(takes_ref, recv_ref, up_ref, down_ref, out_up, out_down, up, down, sems):
    steps = 7
    part = ROWS // steps

    def stores(step):
        rows = pl.ds(step * (part * TALL), part * TALL)
        return (
            pltpu.make_async_copy(up.at[rows], out_up.at[rows], sems.at[0, step]),
            pltpu.make_async_copy(down.at[rows], out_down.at[rows], sems.at[1, step]),
        )

    for step in range(steps):

        def merge(group, carry):
            for r in range(8):
                at = pl.multiple_of(takes_ref[0, group * 8 + r] * (2 * TALL), 2 * TALL)
                where = pl.ds(group * (8 * TALL) + r, TALL, stride=8)
                up[where, :] = (up_ref[where, :] + recv_ref[pl.ds(at, TALL), :]) * 0.5
                down[where, :] = (down_ref[where, :] + recv_ref[pl.ds(at + TALL, TALL), :]) * 0.5
            return carry

        lax.fori_loop(step * (part // 8), (step + 1) * (part // 8), merge, 0)
        for store in stores(step):
            store.start()
    for step in range(steps):
        for store in stores(step):
            store.wait()


def tiles_of(x):
    return x.reshape(ROWS // 8, 8, TALL, 128).transpose(0, 2, 1, 3).reshape(ROWS * TALL, 128)


def rows_of(x):
    return x.reshape(ROWS // 8, TALL, 8, 128).transpose(0, 2, 1, 3).reshape(ROWS, WIDTH)


def on_device(a_up, a_down, b_up, b_down, perm):
    flat = ROWS * TALL
    slots = COUNT * LIMIT * 2 * TALL
    vmem = pl.BlockSpec(memory_space=pltpu.VMEM)
    smem = pl.BlockSpec(memory_space=pltpu.SMEM)
    hbm = pl.BlockSpec(memory_space=pltpu.HBM)
    blocks = perm.reshape(COUNT, ROWS)
    sends, takes = pl.pallas_call(
        tables_kernel,
        name="tables",
        out_shape=(jax.ShapeDtypeStruct((8, 128), jnp.int32), jax.ShapeDtypeStruct((8, 256), jnp.int32)),
        in_specs=[vmem, vmem],
        out_specs=(vmem, vmem),
        cost_estimate=pl.CostEstimate(flops=2_000_000_000, bytes_accessed=1 << 20, transcendentals=0),
        compiler_params=pltpu.CompilerParams(vmem_limit_bytes=4 << 20),
    )(blocks.T, blocks)
    send = pl.pallas_call(
        pack_kernel,
        name="pack",
        out_shape=jax.ShapeDtypeStruct((slots, 128), jnp.float32),
        in_specs=[smem, vmem, vmem],
        out_specs=vmem,
        compiler_params=pltpu.CompilerParams(vmem_limit_bytes=12 << 20),
    )(sends, tiles_of(b_up), tiles_of(b_down))
    recv = lax.all_to_all(
        send.reshape(COUNT, LIMIT * 2 * TALL, 128), EXCHANGE, split_axis=0, concat_axis=0, tiled=True
    ).reshape(slots, 128)
    merged_up, merged_down = pl.pallas_call(
        unpack_kernel,
        name="unpack",
        out_shape=(
            jax.ShapeDtypeStruct((flat, 128), jnp.float32),
            jax.ShapeDtypeStruct((flat, 128), jnp.float32),
        ),
        in_specs=[smem, vmem, vmem, vmem],
        out_specs=(hbm, hbm),
        scratch_shapes=[
            pltpu.VMEM((flat, 128), jnp.float32),
            pltpu.VMEM((flat, 128), jnp.float32),
            pltpu.SemaphoreType.DMA((2, 7)),
        ],
        compiler_params=pltpu.CompilerParams(vmem_limit_bytes=20 << 20),
    )(takes, recv, tiles_of(a_up), tiles_of(a_down))
    return rows_of(merged_up), rows_of(merged_down)


def solution(mesh):
    finer = Mesh(
        mesh.devices.reshape(NX, NZ, NC, mesh.shape["expert"]),
        ("units_0", "units_1", "units_2", "expert"),
    )
    rows = P(EXPERT_UNITS, None)
    return jax.shard_map(
        on_device,
        mesh=finer,
        in_specs=(rows, rows, rows, rows, P("expert")),
        out_specs=(rows, rows),
        check_vma=False,
    )
```

time: 151 us -> 140 us (0.927)
  Pallas kernels: 17.8 us -> 5.24 us
    pallas_call x1 -> x2, Pallas kernels: 8.79 us -> 2.27 us  [the longest x1 2.01 us: on_device(): pl.pallas_call(pack_kernel, name='pack', out_shape=jax.ShapeDtypeStruct((...]
    pallas_call x1, Pallas kernels: 9.01 us -> 2.97 us  [on_device(): pl.pallas_call(unpack_kernel, name='unpack', out_shape=(jax.ShapeDtypeStr...]
    unnamed x0 -> x8, local copies, waits for them, and re-layouts: none -> 1.78 us
where the time goes in v2:
time: 140 us; the launch traced here: 139 us
  blocking collectives  131 us (94%)
  Pallas kernels  5.24 us (4%)
  local copies, waits for them, and re-layouts  2.78 us (2%)
    all_to_all x1, blocking collectives, on_device(): lax.all_to_all(send.reshape(COUNT, LIMIT * 2 * TALL, 128), EXCHANGE, spli...  131 us
    pallas_call x1, Pallas kernels, on_device(): pl.pallas_call(unpack_kernel, name='unpack', out_shape=(jax.ShapeDtypeStr...  2.97 us

profile of v2, /device:TPU:8, one launch (start us, length us, event | category | flops | bytes accessed | tf_op | source)
XLA Modules:
  0.0 139.5 jit_solution(3827498225439256132)
XLA Ops:
  0.6 0.9 reshape.49.blocks_ref
  1.5 0.1 copy.7.perm_ref
  1.6 0.0 copy-start.2
  1.6 0.0 copy-start.3
  1.7 0.3 tables.1
  1.9 1.2 copy-done.2
  3.1 0.6 copy-done.3
  3.7 2.0 %pack.1 = f32[10240,128]{1,0:T(8,128)S(1)} custom-call(s32[8,128]{1,0:T(8,128)S(1)} %get-tuple-element.7.sends_ref, f32[3584,128]{1,0:T(8,128)S(1)} %bitcast.37, f32[3584,128]{1,0:T(8,128)S(1)} %bitcast.38), custom_call_target="tpu_custom_call" | custom-call | tf_op jit(solution)/shard_map/pack/pallas_call | solution.py:127
  5.7 0.0 copy-start
  5.7 0.0 copy-start.1
  5.7 130.8 %all_to_all.5 = f32[64,160,128]{2,1,0:T(8,128)S(1)} all-to-all(f32[64,160,128]{2,1,0:T(8,128)S(1)} %bitcast.34), channel_id=1, replica_groups=mesh['units_0'=4,'units_1'=8,'units_2'=2,'expert'=4] {'units_1','units_2..., dimensions={0} | all-to-all | bytes 10485760 | tf_op jit(solution)/shard_map/all_to_all | solution.py:135
  136.5 0.0 copy-done
  136.5 0.0 copy-done.1
  136.5 3.0 %unpack.1 = (f32[3584,128]{1,0:T(8,128)}, f32[3584,128]{1,0:T(8,128)}) custom-call(s32[8,256]{1,0:T(8,128)S(1)} %get-tuple-element.6.takes_ref, f32[10240,128]{1,0:T(8,128)S(1)} %bitcast.33, f32[3584,128]{1,0:T(8,128)S(1)} %bitcast.35, f32[3584,128]{1,0:T(8,128)S(1)} %bitcast.36), custom_call_target="tpu_custom_call" | custom-call | tf_op jit(solution)/shard_map/unpack/pallas_call | solution.py:138
Async XLA Ops:
  1.6 1.5 %copy-start.2 = (f32[224,2048]{1,0:T(8,128)S(1)}, f32[224,2048]{1,0:T(8,128)}, u32[]{:S(2)}) copy-start(f32[224,2048]{1,0:T(8,128)} %param.7) | copy-start | bytes 5505028
  1.6 2.0 %copy-start.3 = (f32[224,2048]{1,0:T(8,128)S(1)}, f32[224,2048]{1,0:T(8,128)}, u32[]{:S(2)}) copy-start(f32[224,2048]{1,0:T(8,128)} %param.8) | copy-start | bytes 5505028
  5.7 130.8 %copy-start = (f32[224,2048]{1,0:T(8,128)S(1)}, f32[224,2048]{1,0:T(8,128)}, u32[]{:S(2)}) copy-start(f32[224,2048]{1,0:T(8,128)} %param.5) | copy-start | bytes 5505028
  5.7 130.8 %copy-start.1 = (f32[224,2048]{1,0:T(8,128)S(1)}, f32[224,2048]{1,0:T(8,128)}, u32[]{:S(2)}) copy-start(f32[224,2048]{1,0:T(8,128)} %param.6) | copy-start | bytes 5505028
